TPU v7x, 32 devices: a whole 2x2x4 slice. The times are simulated.
32 devices in a mesh: gx: 8 (over y, x, core), gy: 4 (over z).
Axes of the slice: x: 2, y: 2, z: 4, core: 2. Of those that a mesh axis runs over, the one named last changes fastest.
Arguments:
- object_field: float32 [2, 256, 512], P(None, 'gy', 'gx'), may hold values from -1 to 1
- probe_modes: float32 [2, 1024, 128], P(None, ('gy', 'gx')), may hold values from -1.5 to 1.5
- positions: int32 [4, 8, 12, 2], P('gy', 'gx'), may hold values from 4 to 60, as said below
- amplitudes: float32 [4, 8, 12, 128, 128], P('gy', 'gx'), may hold values from 0 to 2
Outputs:
- object_out: float32 [2, 256, 512], P(None, 'gy', 'gx')
- probe_out: float32 [2, 1024, 128], P(None, ('gy', 'gx'))
Inputs may be any that keep to these rules, and one draw needn't show every extreme that they name: `positions`: each entry is a (row, column) inside its own tile; the centres of one tile lie at distinct cells of the 16 grid, each moved from the cell's middle by at most 4 cells along each dimension.
All inputs are finite; a program needn't handle non-finite values.
Results may differ from a plain program's by a relative error of at most 0.00065.
The roundings to bfloat16 on the way count: a program that leaves them out, or rounds other values in their place, can miss the bound.
Values sent between devices are 32-bit elements; how exact they have to be, the bound alone decides.
A program may use at most 64 MiB of HBM per device.

v0:
```python
import math

import jax
import jax.numpy as jnp
from jax import lax
from jax.sharding import PartitionSpec as P

MODES = 8
ITERS = 2


SOFT_FLOOR = 0.05
OBJECT_REG = 1.0
PROBE_REG = 1.0


def from_behind(block, axis, distance):
    devices = range(lax.axis_size(axis))
    route = [(i - distance, i) for i in devices if i - distance in devices]
    return lax.ppermute(block, axis, route)


def extended_2(array, sides, width):
    for axis, dim in sides:
        peers, length = (lax.axis_size(axis), array.shape[dim])
        up = [(i, (i + 1) % peers) for i in range(peers - 1)]
        down = [(j, i) for i, j in up]
        last = lax.slice_in_dim(array, length - width, length, axis=dim)
        initial = lax.slice_in_dim(array, 0, width, axis=dim)
        before = lax.ppermute(last, axis, up)
        after = lax.ppermute(initial, axis, down)
        array = jnp.concatenate([before, array, after], axis=dim)
    return array


def tables(probe_side, sign_flip):
    indices = jnp.arange(probe_side, dtype=jnp.int32)
    phases = indices[:, None] * indices[None, :] % probe_side
    angles = phases.astype(jnp.float32) * (2.0 * math.pi / probe_side)
    factor = 1.0 / math.sqrt(probe_side)
    cosine = jnp.cos(angles) * factor
    sine_part = sign_flip * jnp.sin(angles) * factor
    left_op = jnp.stack(
        [jnp.stack([cosine, -sine_part]), jnp.stack([sine_part, cosine])]
    ).transpose(0, 2, 1, 3)
    right_op = jnp.stack(
        [jnp.stack([cosine, sine_part]), jnp.stack([-sine_part, cosine])]
    ).transpose(0, 2, 1, 3)
    return (left_op.astype(jnp.bfloat16), right_op.astype(jnp.bfloat16))


def transform(signal, operators):
    left_op, right_op = operators
    halfway = jnp.einsum(
        "dpcr,crmq->dpmq", left_op, signal, preferred_element_type=jnp.float32
    ).astype(jnp.bfloat16)
    return jnp.einsum("crmq,cqdk->drmk", halfway, right_op, preferred_element_type=jnp.float32)


def position_terms(patch_obj, probe, measured, forward, inverse):
    obj_real = patch_obj[0][:, None, :]
    obj_imag = patch_obj[1][:, None, :]
    wave_real = probe[0] * obj_real - probe[1] * obj_imag
    wave_imag = probe[0] * obj_imag + probe[1] * obj_real
    signal = jnp.stack([wave_real, wave_imag]).astype(jnp.bfloat16)
    spectrum = transform(signal, forward)
    intensity = jnp.sum(spectrum[0] * spectrum[0] + spectrum[1] * spectrum[1], axis=1)
    shrink = 1.0 - measured / jnp.sqrt(intensity + SOFT_FLOOR)
    residual = (spectrum * shrink[None, :, None, :]).astype(jnp.bfloat16)
    change = transform(residual, inverse)
    grad_real = jnp.sum(probe[0] * change[0] + probe[1] * change[1], axis=1)
    grad_imag = jnp.sum(probe[0] * change[1] - probe[1] * change[0], axis=1)
    probe_real = obj_real * change[0] + obj_imag * change[1]
    probe_imag = obj_real * change[1] - obj_imag * change[0]
    weight_probe = patch_obj[0] * patch_obj[0] + patch_obj[1] * patch_obj[1]
    return (jnp.stack([grad_real, grad_imag]), jnp.stack([probe_real, probe_imag]), weight_probe)


def fold_rows(gradient, margin, tile_side):
    extent = gradient.shape[1]
    for direction in (1, -1):
        rim_part = gradient[:, extent - margin :, :] if direction == 1 else gradient[:, :margin, :]
        offset = margin if direction == 1 else tile_side
        arrived = from_behind(rim_part, "gy", direction)
        gradient = gradient.at[:, offset : offset + margin, :].add(arrived)
    return gradient[:, margin : margin + tile_side, :]


def fold_cols(gradient, margin, tile_side):
    extent = gradient.shape[2]
    for direction in (1, -1):
        rim_part = gradient[:, :, extent - margin :] if direction == 1 else gradient[:, :, :margin]
        offset = margin if direction == 1 else tile_side
        arrived = from_behind(rim_part, "gx", direction)
        gradient = gradient.at[:, :, offset : offset + margin].add(arrived)
    return gradient[:, :, margin : margin + tile_side]


def unpack_probe(probe_rows, probe_side):
    return probe_rows.reshape(2, MODES, probe_side, probe_side).transpose(0, 2, 1, 3)


def local(object_field, probe_modes, positions, amplitudes):
    probe_side = amplitudes.shape[-1]
    margin = probe_side // 2
    tile_side = object_field.shape[1]
    centres = positions.reshape(-1, 2)
    measured_all = amplitudes.reshape(-1, probe_side, probe_side)
    forward = tables(probe_side, -1.0)
    inverse = tables(probe_side, 1.0)
    gathered = lax.all_gather(probe_modes, ("gy", "gx"), axis=1, tiled=True)
    probe = unpack_probe(gathered, probe_side)
    own_rows = probe_modes
    current = object_field
    for iteration in range(ITERS):
        extended = extended_2(current, (("gy", 1), ("gx", 2)), margin)
        weight_obj = jnp.sum(probe[0] * probe[0] + probe[1] * probe[1], axis=1)

        def visit(running, visit_item):
            grad_obj, grad_probe, weight_probe = running
            row_at, col_at, measured = visit_item
            zero_index = jnp.int32(0)
            patch_obj = lax.dynamic_slice(
                extended, (zero_index, row_at, col_at), (2, probe_side, probe_side)
            )
            g_obj, g_probe, w_probe = position_terms(patch_obj, probe, measured, forward, inverse)
            stacked = jnp.concatenate([g_obj, weight_obj[None]], axis=0)
            before = lax.dynamic_slice(
                grad_obj, (zero_index, row_at, col_at), (3, probe_side, probe_side)
            )
            grad_obj = lax.dynamic_update_slice(
                grad_obj, before + stacked, (zero_index, row_at, col_at)
            )
            return ((grad_obj, grad_probe + g_probe, weight_probe + w_probe), None)

        initial = (
            jnp.zeros((3, tile_side + probe_side, tile_side + probe_side), jnp.float32),
            jnp.zeros((2, probe_side, MODES, probe_side), jnp.float32),
            jnp.zeros((probe_side, probe_side), jnp.float32),
        )
        (grad_obj, grad_probe, weight_probe), _ = lax.scan(
            visit, initial, (centres[:, 0], centres[:, 1], measured_all)
        )
        folded = fold_cols(fold_rows(grad_obj, margin, tile_side), margin, tile_side)
        new_object = current - folded[0:2] / (folded[2] + OBJECT_REG)
        grad_rows = grad_probe.transpose(0, 2, 1, 3).reshape(2, MODES * probe_side, probe_side)
        totals, weight_total = lax.psum((grad_rows, weight_probe), ("gy", "gx"))
        whole_probe = probe.transpose(0, 2, 1, 3)
        whole_probe = whole_probe - totals.reshape(2, MODES, probe_side, probe_side) / (
            weight_total[None, None] + PROBE_REG
        )
        whole_probe = whole_probe.reshape(2, MODES * probe_side, probe_side)
        probe = unpack_probe(whole_probe, probe_side)
        row_count = own_rows.shape[1]
        own_rows = lax.dynamic_slice_in_dim(
            whole_probe, lax.axis_index(("gy", "gx")) * row_count, row_count, 1
        )
        current = new_object
    return (current, own_rows)


def solution(mesh):
    return jax.shard_map(
        local,
        mesh=mesh,
        in_specs=(
            P(None, "gy", "gx"),
            P(None, ("gy", "gx"), None),
            P("gy", "gx", None, None),
            P("gy", "gx", None, None, None),
        ),
        out_specs=(P(None, "gy", "gx"), P(None, ("gy", "gx"), None)),
        check_vma=False,
    )
```

profile of v0, /device:TPU:0, one launch (start us, length us, event | category | flops | bytes accessed | tf_op | source)
XLA Modules:
  0.0 768.1 jit_solution(11313479168457631545)
XLA Ops:
  7.9 5.0 collective-permute-start
  22.6 3.1 collective-permute-done.3
  26.6 40.7 %all-gather.2.cloned.1.call-done = f32[2,1024,128]{2,1,0:T(8,128)} async-done(((f32[2,32,128]{2,1,0:T(8,128)}), f32[2,1024,128]{2,1,0:T(8,128)}) %all-gather.2.cloned.1.call-update) | async-done | bytes 1048592 | tf_op jit(solution)/shard_map/all_gather | solution.py:111
  70.1 196.9 %while.38 = (s32[]{:T(128)}, f32[3,192,192]{2,1,0:T(8,128)}, f32[2,128,8,128]{3,1,0,2:T(8,128)}, f32[128,128]{1,0:T(8,128)}, s32[12]{0:T(128)S(1)}, /*index=5*/s...) while((s32[]{:T(128)}, f32[3,192,192]{2,1,0:T(8,128)}, ...), condition=%wide.region_5.6_spmd.clone, body=%wide.region_1.5_spmd.clone.sunk | while | flops 543391744 | bytes 27918840 | solution.py:141
  82.9 2.8 dynamic_update_slice.10
  99.3 2.9 dynamic_update_slice.10
  115.9 2.8 dynamic_update_slice.10
  148.6 2.7 dynamic_update_slice.10
  165.0 2.8 dynamic_update_slice.10
  181.4 2.8 dynamic_update_slice.10
  246.9 2.9 dynamic_update_slice.10
  263.4 2.7 dynamic_update_slice.10
  268.1 3.0 collective-permute-start.4
  272.5 3.2 collective-permute-done.4
  275.6 4.1 collective-permute-done.5
  287.1 2.9 collective-permute-start.8
  291.9 4.3 collective-permute-done.9
  296.2 3.8 collective-permute-start.10
  301.4 2.8 collective-permute-done.11
  305.2 112.8 %all-reduce.7.cloned.1.call-done = (f32[2,1024,128]{2,1,0:T(8,128)}, f32[128,128]{1,0:T(8,128)}) async-done(((f32[2,1024,128]{2,1,0:T(8,128)}, f32[128,128]{1,0:T(8,128)}), (f32[2,1024,128]{2,1,0:T(8,128)}, f32[128,128]{1,0:T(8,128)})) %all-reduce.7.cloned.1.call-update) | async-done | bytes 1114128 | tf_op jit(solution)/shard_map/psum | solution.py:147
  421.8 196.9 %while.39 = (s32[]{:T(128)}, f32[3,192,192]{2,1,0:T(8,128)}, f32[2,128,8,128]{3,1,0,2:T(8,128)}, f32[128,128]{1,0:T(8,128)}, s32[12]{0:T(128)S(1)}, /*index=5*/s...) while((s32[]{:T(128)}, f32[3,192,192]{2,1,0:T(8,128)}, ...), condition=%wide.region_13.14_spmd.clone, body=%wide.region_9.13_spmd.clone.sunk | while | flops 543391744 | bytes 27918840 | solution.py:141
  434.6 2.8 dynamic_update_slice.11
  451.0 2.9 dynamic_update_slice.11
  467.5 2.8 dynamic_update_slice.11
  500.3 2.7 dynamic_update_slice.11
  516.7 2.8 dynamic_update_slice.11
  533.1 2.8 dynamic_update_slice.11
  598.6 2.9 dynamic_update_slice.11
  619.7 4.4 collective-permute-start.12
  627.8 3.9 collective-permute-done.13
  635.4 3.2 collective-permute-done.15
  640.1 119.1 %all-reduce.5.cloned.1.call-done = (f32[2,1024,128]{2,1,0:T(8,128)}, f32[128,128]{1,0:T(8,128)}) async-done(((f32[2,1024,128]{2,1,0:T(8,128)}, f32[128,128]{1,0:T(8,128)}), (f32[2,1024,128]{2,1,0:T(8,128)}, f32[128,128]{1,0:T(8,128)})) %all-reduce.5.cloned.1.call-update) | async-done | bytes 1114128 | tf_op jit(solution)/shard_map/psum | solution.py:147
  (703 shorter events, 315.0 us)
Async XLA Ops:
  7.2 60.0 %all-gather.2.cloned.1.call-start = ((), (), s32[]{:S(2)}) async-start(), calls=%async_computation | async-start | bytes 1081344 | tf_op jit(solution)/shard_map/all_gather | solution.py:111
  7.9 410.0 %all-reduce.7.cloned.1.call-start = ((), (), s32[]{:S(2)}) async-start(), calls=%async_computation.2 | async-start | bytes 2228224 | tf_op jit(solution)/shard_map/psum | solution.py:147
  7.9 8.7 %collective-permute-start = (f32[2,64,64]{2,1,0:T(8,128)}, f32[2,64,64]{2,1,0:T(8,128)S(1)}, u32[]{:S(2)}, u32[]{:S(2)}) collective-permute-start(f32[2,64,64]{2,1,0:T(8,128)} %param.24), channel_id=1, source_target_pairs={{0,1},{1,2},{2,3},{4,5},{5,6},{6,7},{8,9},{9,10},{10,11},{12,13},{... | collective-permute-start | bytes 98312 | tf_op jit(solution)/shard_map/ppermute | solution.py:30
  12.9 6.4 collective-permute-start.1
  19.3 3.3 collective-permute-start.2
  20.6 5.1 collective-permute-start.3
  82.0 3.7 copy-start.1
  98.5 3.7 copy-start.1
  164.1 3.7 copy-start.1
  180.6 3.6 copy-start.1
  246.1 3.7 copy-start.1
  267.0 16.4 %copy-start.2 = (f32[2,128,8,128]{3,1,0,2:T(8,128)S(1)}, f32[2,128,8,128]{3,1,0,2:T(8,128)}, u32[]{:S(2)}) copy-start(f32[2,128,8,128]{3,1,0,2:T(8,128)} %get-tuple-element.247) | copy-start | bytes 3145732
  268.1 7.5 collective-permute-start.4
  271.2 8.6 %collective-permute-start.5 = (f32[3,64,192]{2,1,0:T(8,128)S(1)}, f32[3,64,192]{2,1,0:T(8,128)S(1)}, u32[]{:S(2)}, u32[]{:S(2)}) collective-permute-start(f32[3,64,192]{2,1,0:T(8,128)S(1)} %get-tuple-element.455), channel_id=1, source_target_pairs={{1,0},{2,1},{3,2},{5,4},{6,5},{7,6},{9,8},{10,9},{11,10},{13,12},{... | collective-permute-start | bytes 442376 | tf_op jit(solution)/shard_map/ppermute | solution.py:20
  280.7 3.8 collective-permute-start.6
  282.0 4.9 collective-permute-start.7
  284.5 134.3 %copy-start.13 = (f32[2,1024,128]{2,1,0:T(8,128)S(1)}, f32[2,1024,128]{2,1,0:T(8,128)}, u32[]{:S(2)}) copy-start(f32[2,1024,128]{2,1,0:T(8,128)} %all-gather.2.cloned.1.call-done) | copy-start | bytes 3145732
  284.5 474.7 %all-reduce.5.cloned.1.call-start = ((), (), s32[]{:S(2)}) async-start(), calls=%async_computation.1 | async-start | bytes 2228224 | tf_op jit(solution)/shard_map/psum | solution.py:147
  287.1 17.1 %copy-start.16 = (f32[2,64,64]{2,1,0:T(8,128)}, f32[2,64,64]{2,1,0:T(8,128)S(1)}, u32[]{:S(2)}) copy-start(f32[2,64,64]{2,1,0:T(8,128)S(1)} %fusion.68) | copy-start | bytes 98308
  287.1 4.8 collective-permute-start.8
  290.0 6.2 collective-permute-start.9
  296.2 5.2 collective-permute-start.10
  300.0 4.2 collective-permute-start.11
  433.7 3.7 copy-start.4
  450.2 3.7 copy-start.4
  515.8 3.7 copy-start.4
  532.3 3.6 copy-start.4
  597.8 3.7 copy-start.4
  619.7 8.0 %collective-permute-start.12 = (f32[3,64,192]{2,1,0:T(8,128)S(1)}, f32[3,64,192]{2,1,0:T(8,128)S(1)}, u32[]{:S(2)}, u32[]{:S(2)}) collective-permute-start(f32[3,64,192]{2,1,0:T(8,128)S(1)} %get-tuple-element.452), channel_id=1, source_target_pairs={{0,1},{1,2},{2,3},{4,5},{5,6},{6,7},{8,9},{9,10},{10,11},{12,13},{... | collective-permute-start | bytes 442376 | tf_op jit(solution)/shard_map/ppermute | solution.py:20
  624.1 7.6 collective-permute-start.13
  632.7 2.7 collective-permute-start.14
  634.0 4.5 collective-permute-start.15
  (164 other events, 191.5 us)
Sparse Core Ops, SparseCore 0:
  10.9 56.2 all-gather.1
  284.6 133.3 all-reduce.6
  627.9 131.2 all-reduce.4
where the time goes:
time: 773 us; the launch traced here: 768 us
  waiting for transfers between devices  303 us (39%)
  local copies, waits for them, and re-layouts  154 us (20%)
  other arithmetic  137 us (18%)
  loops' own time  80.7 us (10%)
  matrix products  46.8 us (6%)
  starting transfers between devices  33.4 us (4%)
  between operations  14.2 us (2%)
    psum x2, waiting for transfers between devices, local(): totals, weight_total = lax.psum((grad_rows, weight_probe), ('gy', 'gx'))  232 us
    another operation x2, loops' own time, local(): lax.scan(visit, initial, (centres[:, 0], centres[:, 1], measured_all))  80.7 us
    dynamic_update_slice x24, local copies, waits for them, and re-layouts, visit(): lax.dynamic_update_slice(grad_obj, before + stacked, (zero_index, row_at,...  66.2 us
    add x48, other arithmetic, visit(): return ((grad_obj, grad_probe + g_probe, weight_probe + w_probe), None)  50.6 us
    while x336, local copies, waits for them, and re-layouts  49.5 us
    dot_general x48, matrix products, transform(): jnp.einsum('crmq,cqdk->drmk', halfway, right_op, preferred_element_type=j...  46.8 us
    all_gather x1, waiting for transfers between devices, local(): gathered = lax.all_gather(probe_modes, ('gy', 'gx'), axis=1, tiled=True)  40.7 us
    sub x24, other arithmetic, position_terms(): shrink = 1.0 - measured / jnp.sqrt(intensity + SOFT_FLOOR)  35.8 us
  transfers between devices with their start and end apart: 19, of which 13 were waited for; matrix products, arithmetic and copies ran while one was open for 1% of the time, Pallas kernels for 0%

commit v1 on v0

v1 whole, which is shorter than its diff:
```python
import math

import jax
import jax.numpy as jnp
from jax import lax
from jax.experimental import pallas as pl
from jax.experimental.pallas import tpu as pltpu
from jax.sharding import PartitionSpec as P

MODES = 8
ITERS = 2
SUBLANES = 8


SOFT_FLOOR = 0.05
OBJECT_REG = 1.0
PROBE_REG = 1.0


def from_behind(block, axis, distance):
    devices = range(lax.axis_size(axis))
    route = [(i - distance, i) for i in devices if i - distance in devices]
    return lax.ppermute(block, axis, route)


def extended_2(array, sides, width):
    for axis, dim in sides:
        peers, length = (lax.axis_size(axis), array.shape[dim])
        up = [(i, (i + 1) % peers) for i in range(peers - 1)]
        down = [(j, i) for i, j in up]
        last = lax.slice_in_dim(array, length - width, length, axis=dim)
        initial = lax.slice_in_dim(array, 0, width, axis=dim)
        before = lax.ppermute(last, axis, up)
        after = lax.ppermute(initial, axis, down)
        array = jnp.concatenate([before, array, after], axis=dim)
    return array


def tables(probe_side, sign_flip):
    indices = jnp.arange(probe_side, dtype=jnp.int32)
    phases = indices[:, None] * indices[None, :] % probe_side
    angles = phases.astype(jnp.float32) * (2.0 * math.pi / probe_side)
    factor = 1.0 / math.sqrt(probe_side)
    cosine = jnp.cos(angles) * factor
    sine_part = sign_flip * jnp.sin(angles) * factor
    left_op = jnp.stack(
        [jnp.stack([cosine, -sine_part]), jnp.stack([sine_part, cosine])]
    ).transpose(0, 2, 1, 3)
    right_op = jnp.stack(
        [jnp.stack([cosine, sine_part]), jnp.stack([-sine_part, cosine])]
    ).transpose(0, 2, 1, 3)
    return (left_op.astype(jnp.bfloat16), right_op.astype(jnp.bfloat16))


def visit_kernel(places, ext_ref, probe_ref, measured_ref, fwd_left, fwd_right, inv_left, inv_right,
                 grad_obj_ref, grad_probe_ref, weight_probe_ref, far_ref, weight_obj_ref):
    count, side, _ = measured_ref.shape
    modes = probe_ref.shape[1] // side
    lanes = ext_ref.shape[2]
    grad_obj_ref[...] = jnp.zeros_like(grad_obj_ref)
    grad_probe_ref[...] = jnp.zeros_like(grad_probe_ref)
    weight_probe_ref[...] = jnp.zeros_like(weight_probe_ref)
    weight = jnp.zeros((side, side), jnp.float32)
    for m in range(modes):
        p_real = probe_ref[0, m * side : (m + 1) * side, :]
        p_imag = probe_ref[1, m * side : (m + 1) * side, :]
        weight += p_real * p_real + p_imag * p_imag
    weight_obj_ref[...] = weight

    def dot(left, right):
        return jnp.dot(left, right, preferred_element_type=jnp.float32)

    def two_sided(left_op, right_op, pair):
        half = dot(left_op[...], pair).astype(jnp.bfloat16)
        results = []
        for k in range(2):
            block = half[:, k * side : (k + 1) * side]
            rows = jnp.concatenate([block[:side], block[side:]], axis=1)
            results.append(dot(rows, right_op[...]))
        return results

    def visit(j, carry):
        row_at = places[j, 0]
        col_at = places[j, 1]
        tall = side + SUBLANES
        shift = lax.rem(row_at, SUBLANES)
        window = pl.ds(pl.multiple_of(row_at - shift, SUBLANES), tall)
        right = lax.rem(lanes - col_at, lanes)
        up = lax.rem(tall - shift, tall)

        def patch_of(i):
            columns = pltpu.roll(ext_ref[i, window, :], right, 1)[:, :side]
            return pltpu.roll(columns, up, 0)[:side]

        o_real = patch_of(0)
        o_imag = patch_of(1)
        weight_probe_ref[...] += o_real * o_real + o_imag * o_imag
        intensity = jnp.zeros((side, side), jnp.float32)
        for m in range(0, modes, 2):
            columns = []
            for k in (m, m + 1):
                p_real = probe_ref[0, k * side : (k + 1) * side, :]
                p_imag = probe_ref[1, k * side : (k + 1) * side, :]
                w_real = (p_real * o_real - p_imag * o_imag).astype(jnp.bfloat16)
                w_imag = (p_real * o_imag + p_imag * o_real).astype(jnp.bfloat16)
                columns.append(jnp.concatenate([w_real, w_imag], axis=0))
            for k, far in enumerate(two_sided(fwd_left, fwd_right, jnp.concatenate(columns, axis=1))):
                far_ref[(m + k) * side : (m + k + 1) * side, :] = far
                intensity += far[:, :side] * far[:, :side] + far[:, side:] * far[:, side:]
        shrink = 1.0 - measured_ref[j] / jnp.sqrt(intensity + SOFT_FLOOR)
        g_real = jnp.zeros((side, side), jnp.float32)
        g_imag = jnp.zeros((side, side), jnp.float32)
        for m in range(0, modes, 2):
            columns = []
            for k in (m, m + 1):
                rows = slice(k * side, (k + 1) * side)
                r_real = (far_ref[rows, :side] * shrink).astype(jnp.bfloat16)
                r_imag = (far_ref[rows, side:] * shrink).astype(jnp.bfloat16)
                columns.append(jnp.concatenate([r_real, r_imag], axis=0))
            for k, change in enumerate(two_sided(inv_left, inv_right, jnp.concatenate(columns, axis=1))):
                rows = slice((m + k) * side, (m + k + 1) * side)
                p_real = probe_ref[0, rows, :]
                p_imag = probe_ref[1, rows, :]
                c_real = change[:, :side]
                c_imag = change[:, side:]
                g_real += p_real * c_real + p_imag * c_imag
                g_imag += p_real * c_imag - p_imag * c_real
                grad_probe_ref[0, rows, :] += o_real * c_real + o_imag * c_imag
                grad_probe_ref[1, rows, :] += o_real * c_imag - o_imag * c_real
        short = jnp.zeros((SUBLANES, side), jnp.float32)
        blank = jnp.zeros((tall, lanes - side), jnp.float32)
        for i, part in enumerate((g_real, g_imag, weight_obj_ref[...])):
            part = jnp.concatenate([part, short], axis=0)
            wide = jnp.concatenate([pltpu.roll(part, shift, 0), blank], axis=1)
            grad_obj_ref[i, window, :] += pltpu.roll(wide, col_at, 1)
        return carry

    lax.fori_loop(0, count, visit, 0)


def flat(operators):
    left_op, right_op = operators
    side = left_op.shape[1]
    return (left_op.reshape(2 * side, 2 * side), right_op.reshape(2 * side, 2 * side))


def gradients(extended, probe, places, measured, forward, inverse):
    side = measured.shape[-1]
    vmem = pl.BlockSpec(memory_space=pltpu.VMEM)
    rows, lanes = extended.shape[1:]
    flops = measured.shape[0] * 4 * 2 * (2 * side) ** 2 * probe.shape[1]
    return pl.pallas_call(
        visit_kernel,
        out_shape=(
            jax.ShapeDtypeStruct((3, rows, lanes), jnp.float32),
            jax.ShapeDtypeStruct(probe.shape, jnp.float32),
            jax.ShapeDtypeStruct((side, side), jnp.float32),
        ),
        in_specs=[pl.BlockSpec(memory_space=pltpu.SMEM)] + [vmem] * 7,
        out_specs=(vmem, vmem, vmem),
        scratch_shapes=[
            pltpu.VMEM((probe.shape[1], 2 * side), jnp.float32),
            pltpu.VMEM((side, side), jnp.float32),
        ],
        compiler_params=pltpu.CompilerParams(vmem_limit_bytes=32 * 1024 * 1024),
        cost_estimate=pl.CostEstimate(flops=flops, bytes_accessed=4 * 1024 * 1024, transcendentals=0),
        name="visits",
    )(places, extended, probe, measured, *forward, *inverse)


def fold_rows(gradient, margin, tile_side):
    extent = gradient.shape[1]
    for direction in (1, -1):
        rim_part = gradient[:, extent - margin :, :] if direction == 1 else gradient[:, :margin, :]
        offset = margin if direction == 1 else tile_side
        arrived = from_behind(rim_part, "gy", direction)
        gradient = gradient.at[:, offset : offset + margin, :].add(arrived)
    return gradient[:, margin : margin + tile_side, :]


def fold_cols(gradient, margin, tile_side):
    extent = gradient.shape[2]
    for direction in (1, -1):
        rim_part = gradient[:, :, extent - margin :] if direction == 1 else gradient[:, :, :margin]
        offset = margin if direction == 1 else tile_side
        arrived = from_behind(rim_part, "gx", direction)
        gradient = gradient.at[:, :, offset : offset + margin].add(arrived)
    return gradient[:, :, margin : margin + tile_side]


def whole_of(own):
    planes = []
    for plane in own:
        planes.append(lax.all_gather(plane, ("gy", "gx"), axis=0, tiled=True))
        own = lax.optimization_barrier(own)
    return jnp.stack(planes)


def scattered_sum(terms):
    planes, rows, side = terms.shape
    down, across = lax.axis_size("gy"), lax.axis_size("gx")
    terms = terms.reshape(planes, down, across, rows // (down * across), side)
    terms = terms.transpose(2, 0, 1, 3, 4)
    terms = lax.all_to_all(terms, "gx", 0, 0, tiled=True).sum(axis=0)
    terms = terms.transpose(1, 0, 2, 3)
    return lax.all_to_all(terms, "gy", 0, 0, tiled=True).sum(axis=0)


def local(object_field, probe_modes, positions, amplitudes):
    probe_side = amplitudes.shape[-1]
    margin = probe_side // 2
    tile_side = object_field.shape[1]
    lanes = -(-(tile_side + probe_side) // 128) * 128
    places = positions.reshape(-1, 2)
    measured = amplitudes.reshape(-1, probe_side, probe_side)
    forward = flat(tables(probe_side, -1.0))
    inverse = flat(tables(probe_side, 1.0))
    own = probe_modes
    probe = whole_of(own)
    current = object_field
    for iteration in range(ITERS):
        extended = extended_2(current, (("gy", 1), ("gx", 2)), margin)
        extended = jnp.pad(extended, ((0, 0), (0, 0), (0, lanes - extended.shape[2])))
        grad_obj, grad_probe, weight_probe = gradients(
            extended, probe, places, measured, forward, inverse
        )
        grad_obj = grad_obj[:, :, : tile_side + probe_side]
        folded = fold_cols(fold_rows(grad_obj, margin, tile_side), margin, tile_side)
        current = current - folded[0:2] / (folded[2] + OBJECT_REG)
        weights = jnp.tile(weight_probe, (MODES, 1))[None]
        totals = scattered_sum(jnp.concatenate([grad_probe, weights]))
        own = own - totals[0:2] / (totals[2:3] + PROBE_REG)
        if iteration < ITERS - 1:
            probe = whole_of(own)
    return (current, own)


def solution(mesh):
    return jax.shard_map(
        local,
        mesh=mesh,
        in_specs=(
            P(None, "gy", "gx"),
            P(None, ("gy", "gx"), None),
            P("gy", "gx", None, None),
            P("gy", "gx", None, None, None),
        ),
        out_specs=(P(None, "gy", "gx"), P(None, ("gy", "gx"), None)),
        check_vma=False,
    )
```

time: 773 us -> 313 us (0.40)
  waiting for transfers between devices: 303 us -> 35.8 us
  blocking collectives: 0 us -> 165 us
  local copies, waits for them, and re-layouts: 154 us -> 3.05 us
  other arithmetic: 137 us -> 7.9 us
  loops' own time: 80.7 us -> 0 us
  matrix products: 46.8 us -> 0 us
  Pallas kernels: 0 us -> 40 us
  starting transfers between devices: 33.4 us -> 59.1 us
  between operations: 14.2 us -> 1.22 us
    psum x2 -> x0, waiting for transfers between devices: 232 us -> none  [local(): totals, weight_total = lax.psum((grad_rows, weight_probe), ('gy', 'gx'))]
    all_gather x0 -> x4, blocking collectives: none -> 165 us  [whole_of(): planes.append(lax.all_gather(plane, ('gy', 'gx'), axis=0, tiled=True))]
    add x98 -> x0, other arithmetic: 84.6 us -> none  [the longest x48 50.6 us: visit(): return ((grad_obj, grad_probe + g_probe, weight_probe + w_probe), None)]
    another operation x2 -> x0, loops' own time: 80.7 us -> none  [local(): lax.scan(visit, initial, (centres[:, 0], centres[:, 1], measured_all))]
    dynamic_update_slice x24 -> x0, local copies, waits for them, and re-layouts: 66.2 us -> none  [visit(): lax.dynamic_update_slice(grad_obj, before + stacked, (zero_index, row_at,...]
    while x336 -> x0, local copies, waits for them, and re-layouts: 49.5 us -> none
    dot_general x48 -> x0, matrix products: 46.8 us -> none  [transform(): jnp.einsum('crmq,cqdk->drmk', halfway, right_op, preferred_element_type=j...]
    all_gather x1 -> x0, waiting for transfers between devices: 40.7 us -> none  [local(): gathered = lax.all_gather(probe_modes, ('gy', 'gx'), axis=1, tiled=True)]
  transfers between devices with their start and end apart: 19 -> 20, of which waited for: 13 -> 9; matrix products, arithmetic and copies ran while one was open for 1% -> 2% of each run, Pallas kernels for 0% -> 0%
where the time goes in v1:
time: 313 us; the launch traced here: 312 us
  blocking collectives  165 us (53%)
  starting transfers between devices  59.1 us (19%)
  Pallas kernels  40 us (13%)
  waiting for transfers between devices  35.8 us (11%)
  other arithmetic  7.9 us (3%)
    all_gather x4, blocking collectives, whole_of(): planes.append(lax.all_gather(plane, ('gy', 'gx'), axis=0, tiled=True))  165 us
    pallas_call x2, Pallas kernels, gradients(): pl.pallas_call(visit_kernel, out_shape=(jax.ShapeDtypeStruct((3, rows, la...  40 us
    ppermute x4, starting transfers between devices, extended_2(): before = lax.ppermute(last, axis, up)  22.5 us
    ppermute x8, waiting for transfers between devices, from_behind(): return lax.ppermute(block, axis, route)  15.4 us
    all_to_all x2, starting transfers between devices, scattered_sum(): terms = lax.all_to_all(terms, 'gx', 0, 0, tiled=True).sum(axis=0)  12.4 us
    ppermute x8, starting transfers between devices, from_behind(): return lax.ppermute(block, axis, route)  11.6 us
    all_to_all x2, waiting for transfers between devices, scattered_sum(): terms = lax.all_to_all(terms, 'gx', 0, 0, tiled=True).sum(axis=0)  11.3 us
    all_to_all x2, starting transfers between devices, scattered_sum(): return lax.all_to_all(terms, 'gy', 0, 0, tiled=True).sum(axis=0)  7.28 us
  transfers between devices with their start and end apart: 20, of which 9 were waited for; matrix products, arithmetic and copies ran while one was open for 2% of the time, Pallas kernels for 0%

profile of v1, /device:TPU:0, one launch (start us, length us, event | category | flops | bytes accessed | tf_op | source)
XLA Modules:
  0.0 312.1 jit_solution(5762584293659237952)
XLA Ops:
  0.6 1.3 collective-permute-start.1
  1.9 5.6 %collective-permute-start = (f32[2,64,64]{2,1,0:T(8,128)}, f32[2,64,64]{2,1,0:T(8,128)S(1)}, u32[]{:S(2)}, u32[]{:S(2)}) collective-permute-start(f32[2,64,64]{2,1,0:T(8,128)} %param.20), channel_id=1, source_target_pairs={{0,1},{1,2},{2,3},{4,5},{5,6},{6,7},{8,9},{9,10},{10,11},{12,13},{... | collective-permute-start | bytes 98312 | tf_op jit(solution)/shard_map/ppermute | solution.py:33
  9.6 41.5 %all-gather = f32[1,1024,128]{2,1,0:T(8,128)S(1)} all-gather(f32[1,32,128]{2,1,0:T(8,128)S(1)} %get-tuple-element.134), channel_id=2, replica_groups=mesh['gx'=8,'gy'=4] {'gy','gx'}, dimensions={1}, use_global_device_ids=true | all-gather | bytes 540672 | tf_op jit(solution)/shard_map/all_gather | solution.py:194
  51.1 38.0 %all-gather.1 = f32[1,1024,128]{2,1,0:T(8,128)S(1)} all-gather(f32[1,32,128]{2,1,0:T(8,128)S(1)} %get-tuple-element.135), channel_id=3, replica_groups=mesh['gx'=8,'gy'=4] {'gy','gx'}, dimensions={1}, use_global_device_ids=true | all-gather | bytes 540672 | tf_op jit(solution)/shard_map/all_gather | solution.py:194
  90.2 1.4 collective-permute-start.3
  91.6 3.0 collective-permute-start.2
  95.9 20.0 %visits.2 = (f32[3,192,256]{2,1,0:T(8,128)S(1)}, f32[2,1024,128]{2,1,0:T(8,128)S(1)}, f32[128,128]{1,0:T(8,128)S(1)}) custom-call(s32[12,2]{1,0:T(8,128)S(1)} %copy.30.places, f32[2,192,256]{2,1,0:T(8,128)S(1)} %select_maximum_fusion.4.ext_ref, f32[2,1024,128]{2,1,0:T(8,128)S(1)} %pad_maximum_fusion.2.probe_ref, f32[12,128,128]{2,1,0:T(8,128)S(1)} %bitcast.74, ...), custom_call_target="tpu_custom_call" | custom-call | flops 6442450944 | bytes 4194304 | tf_op jit(solution)/shard_map/visits/pallas_call | solution.py:152
  115.9 1.3 collective-permute-start.4
  118.6 1.3 copy_bitcast_fusion.1
  119.9 8.8 %all-to-all-start = ((f32[8,3,4,32,128]{4,3,2,1,0:T(8,128)}), f32[8,3,4,32,128]{4,3,2,1,0:T(8,128)}, u32[]{:S(2)}, u32[]{:S(2)}) async-start(f32[8,3,4,32,128]{4,3,2,1,0:T(8,128)} %copy_bitcast_fusion.1), calls=%async_computation | async-start | bytes 3145728 | tf_op jit(solution)/shard_map/all_to_all | solution.py:204
  128.8 2.4 collective-permute-start.6
  132.5 3.9 %collective-permute-done.7 = f32[3,64,64]{2,1,0:T(8,128)S(1)} collective-permute-done((f32[3,64,64]{2,1,0:T(8,128)S(1)}, f32[3,64,64]{2,1,0:T(8,128)S(1)}, u32[]{:S(2)}, u32[]{:S(2)}) %collective-permute-start.7) | collective-permute-done | bytes 49184 | tf_op jit(solution)/shard_map/ppermute | solution.py:23
  137.9 4.5 %collective-permute-start.8 = (f32[2,64,64]{2,1,0:T(8,128)S(1)}, f32[2,64,64]{2,1,0:T(8,128)S(1)}, u32[]{:S(2)}, u32[]{:S(2)}) collective-permute-start(f32[2,64,64]{2,1,0:T(8,128)S(1)} %fusion.14), channel_id=1, source_target_pairs={{0,1},{1,2},{2,3},{4,5},{5,6},{6,7},{8,9},{9,10},{10,11},{12,13},{... | collective-permute-start | bytes 98312 | tf_op jit(solution)/shard_map/ppermute | solution.py:33
  142.5 7.4 %all-to-all-done = f32[8,3,4,32,128]{4,3,2,1,0:T(8,128)} async-done(((f32[8,3,4,32,128]{4,3,2,1,0:T(8,128)}), f32[8,3,4,32,128]{4,3,2,1,0:T(8,128)}, u32[]{:S(2)}, u32[]{:S(2)}) %all-to-all-start) | async-done | bytes 1572896 | tf_op jit(solution)/shard_map/all_to_all | solution.py:204
  149.8 1.6 reduce_sum.36
  152.1 3.9 %all-to-all-start.1 = ((f32[4,3,32,128]{3,2,1,0:T(8,128)}), f32[4,3,32,128]{3,2,1,0:T(8,128)S(1)}, u32[]{:S(2)}, u32[]{:S(2)}) async-start(f32[4,3,32,128]{3,2,1,0:T(8,128)} %copy.33), calls=%async_computation.1 | async-start | bytes 393216 | tf_op jit(solution)/shard_map/all_to_all | solution.py:206
  156.0 1.3 collective-permute-start.11
  157.3 9.3 %collective-permute-start.10 = (f32[2,192,64]{2,1,0:T(8,128)S(1)}, f32[2,192,64]{2,1,0:T(8,128)S(1)}, u32[]{:S(2)}, u32[]{:S(2)}) collective-permute-start(f32[2,192,64]{2,1,0:T(8,128)S(1)} %pad_maximum_fusion.4), channel_id=1, source_target_pairs={{0,4},{4,8},{8,12},{12,16},{16,20},{20,24},{24,28},{1,5},{5,9},{9,... | collective-permute-start | bytes 294920 | tf_op jit(solution)/shard_map/ppermute | solution.py:33
  168.0 47.4 %all-gather.2 = f32[1,1024,128]{2,1,0:T(8,128)S(1)} all-gather(f32[1,32,128]{2,1,0:T(8,128)S(1)} %get-tuple-element.126), channel_id=4, replica_groups=mesh['gx'=8,'gy'=4] {'gy','gx'}, dimensions={1}, use_global_device_ids=true | all-gather | bytes 540672 | tf_op jit(solution)/shard_map/all_gather | solution.py:194
  215.4 38.0 %all-gather.3 = f32[1,1024,128]{2,1,0:T(8,128)S(1)} all-gather(f32[1,32,128]{2,1,0:T(8,128)S(1)} %get-tuple-element.127), channel_id=5, replica_groups=mesh['gx'=8,'gy'=4] {'gy','gx'}, dimensions={1}, use_global_device_ids=true | all-gather | bytes 540672 | tf_op jit(solution)/shard_map/all_gather | solution.py:194
  253.5 20.0 %visits.3 = (f32[3,192,256]{2,1,0:T(8,128)S(1)}, f32[2,1024,128]{2,1,0:T(8,128)S(1)}, f32[128,128]{1,0:T(8,128)S(1)}) custom-call(s32[12,2]{1,0:T(8,128)S(1)} %copy.30.places, f32[2,192,256]{2,1,0:T(8,128)S(1)} %select_maximum_fusion.ext_ref, f32[2,1024,128]{2,1,0:T(8,128)S(1)} %pad_maximum_fusion.3.probe_ref, f32[12,128,128]{2,1,0:T(8,128)S(1)} %bitcast.75, ...), custom_call_target="tpu_custom_call" | custom-call | flops 6442450944 | bytes 4194304 | tf_op jit(solution)/shard_map/visits/pallas_call | solution.py:152
  273.5 1.3 copy_bitcast_fusion
  274.9 3.6 %all-to-all-start.2 = ((f32[8,3,4,32,128]{4,3,2,1,0:T(8,128)}), f32[8,3,4,32,128]{4,3,2,1,0:T(8,128)S(1)}, u32[]{:S(2)}, u32[]{:S(2)}) async-start(f32[8,3,4,32,128]{4,3,2,1,0:T(8,128)} %copy_bitcast_fusion), calls=%async_computation.2 | async-start | bytes 3145728 | tf_op jit(solution)/shard_map/all_to_all | solution.py:204
  278.5 1.3 collective-permute-start.12
  279.8 1.3 collective-permute-start.13
  281.1 3.7 %collective-permute-done.12 = f32[3,64,192]{2,1,0:T(8,128)S(1)} collective-permute-done((f32[3,64,192]{2,1,0:T(8,128)S(1)}, f32[3,64,192]{2,1,0:T(8,128)S(1)}, u32[]{:S(2)}, u32[]{:S(2)}) %collective-permute-start.12) | collective-permute-done | bytes 147488 | tf_op jit(solution)/shard_map/ppermute | solution.py:23
  284.8 4.1 %collective-permute-done.13 = f32[3,64,192]{2,1,0:T(8,128)S(1)} collective-permute-done((f32[3,64,192]{2,1,0:T(8,128)S(1)}, f32[3,64,192]{2,1,0:T(8,128)S(1)}, u32[]{:S(2)}, u32[]{:S(2)}) %collective-permute-start.13) | collective-permute-done | bytes 147488 | tf_op jit(solution)/shard_map/ppermute | solution.py:23
  289.0 1.4 collective-permute-start.14
  291.8 3.6 %collective-permute-done.15 = f32[3,64,64]{2,1,0:T(8,128)S(1)} collective-permute-done((f32[3,64,64]{2,1,0:T(8,128)S(1)}, f32[3,64,64]{2,1,0:T(8,128)S(1)}, u32[]{:S(2)}, u32[]{:S(2)}) %collective-permute-start.15) | collective-permute-done | bytes 49184 | tf_op jit(solution)/shard_map/ppermute | solution.py:23
  295.5 3.9 %all-to-all-done.2 = f32[8,3,4,32,128]{4,3,2,1,0:T(8,128)S(1)} async-done(((f32[8,3,4,32,128]{4,3,2,1,0:T(8,128)}), f32[8,3,4,32,128]{4,3,2,1,0:T(8,128)S(1)}, u32[]{:S(2)}, u32[]{:S(2)}) %all-to-all-start.2) | async-done | bytes 1572896 | tf_op jit(solution)/shard_map/all_to_all | solution.py:204
  300.2 3.4 %all-to-all-start.3 = ((f32[4,3,32,128]{3,2,1,0:T(8,128)}), f32[4,3,32,128]{3,2,1,0:T(8,128)S(1)}, u32[]{:S(2)}, u32[]{:S(2)}) async-start(f32[4,3,32,128]{3,2,1,0:T(8,128)} %copy.37), calls=%async_computation.3 | async-start | bytes 393216 | tf_op jit(solution)/shard_map/all_to_all | solution.py:206
  304.3 7.1 %all-to-all-done.3 = f32[4,3,32,128]{3,2,1,0:T(8,128)S(1)} async-done(((f32[4,3,32,128]{3,2,1,0:T(8,128)}), f32[4,3,32,128]{3,2,1,0:T(8,128)S(1)}, u32[]{:S(2)}, u32[]{:S(2)}) %all-to-all-start.3) | async-done | bytes 196640 | tf_op jit(solution)/shard_map/all_to_all | solution.py:206
  (75 shorter events, 13.9 us)
Async XLA Ops:
  0.6 88.7 %copy-start.3 = (s32[1,1,12,2]{2,3,1,0:T(2,128)S(1)}, s32[1,1,12,2]{2,3,1,0:T(2,128)}, u32[]{:S(2)}) copy-start(s32[1,1,12,2]{2,3,1,0:T(2,128)} %param.22) | copy-start | bytes 292
  0.6 89.5 %collective-permute-start.1 = (f32[2,64,64]{2,1,0:T(8,128)}, f32[2,64,64]{2,1,0:T(8,128)S(1)}, u32[]{:S(2)}, u32[]{:S(2)}) collective-permute-start(f32[2,64,64]{2,1,0:T(8,128)} %param.20), channel_id=1, source_target_pairs={{1,0},{2,1},{3,2},{5,4},{6,5},{7,6},{9,8},{10,9},{11,10},{13,12},{... | collective-permute-start | bytes 98312 | tf_op jit(solution)/shard_map/ppermute | solution.py:34
  1.9 88.2 %collective-permute-start = (f32[2,64,64]{2,1,0:T(8,128)}, f32[2,64,64]{2,1,0:T(8,128)S(1)}, u32[]{:S(2)}, u32[]{:S(2)}) collective-permute-start(f32[2,64,64]{2,1,0:T(8,128)} %param.20), channel_id=1, source_target_pairs={{0,1},{1,2},{2,3},{4,5},{5,6},{6,7},{8,9},{9,10},{10,11},{12,13},{... | collective-permute-start | bytes 98312 | tf_op jit(solution)/shard_map/ppermute | solution.py:33
  89.2 0.9 copy-start.1
  90.2 5.7 %copy-start = (f32[1,1,12,128,128]{4,3,2,1,0:T(8,128)S(1)}, f32[1,1,12,128,128]{4,3,2,1,0:T(8,128)}, u32[]{:S(2)}) copy-start(f32[1,1,12,128,128]{4,3,2,1,0:T(8,128)} %param.23) | copy-start | bytes 2359300
  90.2 4.6 %collective-permute-start.3 = (f32[2,192,64]{2,1,0:T(8,128)S(1)}, f32[2,192,64]{2,1,0:T(8,128)S(1)}, u32[]{:S(2)}, u32[]{:S(2)}) collective-permute-start(f32[2,192,64]{2,1,0:T(8,128)S(1)} %constant_dynamic-update-slice_fusion), channel_id=1, source_target_pairs={{4,0},{8,4},{12,8},{16,12},{20,16},{24,20},{28,24},{5,1},{9,5},{13... | collective-permute-start | bytes 294920 | tf_op jit(solution)/shard_map/ppermute | solution.py:34
  91.6 4.1 %collective-permute-start.2 = (f32[2,192,64]{2,1,0:T(8,128)S(1)}, f32[2,192,64]{2,1,0:T(8,128)S(1)}, u32[]{:S(2)}, u32[]{:S(2)}) collective-permute-start(f32[2,192,64]{2,1,0:T(8,128)S(1)} %constant_dynamic-update-slice_fusion), channel_id=1, source_target_pairs={{0,4},{4,8},{8,12},{12,16},{16,20},{20,24},{24,28},{1,5},{5,9},{9,... | collective-permute-start | bytes 294920 | tf_op jit(solution)/shard_map/ppermute | solution.py:33
  115.9 12.8 %collective-permute-start.4 = (f32[3,64,192]{2,1,0:T(8,128)S(1)}, f32[3,64,192]{2,1,0:T(8,128)S(1)}, u32[]{:S(2)}, u32[]{:S(2)}) collective-permute-start(f32[3,64,192]{2,1,0:T(8,128)S(1)} %get-tuple-element.112), channel_id=1, source_target_pairs={{0,1},{1,2},{2,3},{4,5},{5,6},{6,7},{8,9},{9,10},{10,11},{12,13},{... | collective-permute-start | bytes 442376 | tf_op jit(solution)/shard_map/ppermute | solution.py:23
  117.2 11.5 %collective-permute-start.5 = (f32[3,64,192]{2,1,0:T(8,128)S(1)}, f32[3,64,192]{2,1,0:T(8,128)S(1)}, u32[]{:S(2)}, u32[]{:S(2)}) collective-permute-start(f32[3,64,192]{2,1,0:T(8,128)S(1)} %get-tuple-element.113), channel_id=1, source_target_pairs={{1,0},{2,1},{3,2},{5,4},{6,5},{7,6},{9,8},{10,9},{11,10},{13,12},{... | collective-permute-start | bytes 442376 | tf_op jit(solution)/shard_map/ppermute | solution.py:23
  119.9 29.9 %all-to-all-start = ((f32[8,3,4,32,128]{4,3,2,1,0:T(8,128)}), f32[8,3,4,32,128]{4,3,2,1,0:T(8,128)}, u32[]{:S(2)}, u32[]{:S(2)}) async-start(f32[8,3,4,32,128]{4,3,2,1,0:T(8,128)} %copy_bitcast_fusion.1), calls=%async_computation | async-start | bytes 3145728 | tf_op jit(solution)/shard_map/all_to_all | solution.py:204
  128.8 3.7 %collective-permute-start.6 = (f32[3,64,64]{2,1,0:T(8,128)S(1)}, f32[3,64,64]{2,1,0:T(8,128)S(1)}, u32[]{:S(2)}, u32[]{:S(2)}) collective-permute-start(f32[3,64,64]{2,1,0:T(8,128)S(1)} %get-tuple-element.116), channel_id=1, source_target_pairs={{0,4},{4,8},{8,12},{12,16},{16,20},{20,24},{24,28},{1,5},{5,9},{9,... | collective-permute-start | bytes 147464 | tf_op jit(solution)/shard_map/ppermute | solution.py:23
  131.2 5.2 %collective-permute-start.7 = (f32[3,64,64]{2,1,0:T(8,128)S(1)}, f32[3,64,64]{2,1,0:T(8,128)S(1)}, u32[]{:S(2)}, u32[]{:S(2)}) collective-permute-start(f32[3,64,64]{2,1,0:T(8,128)S(1)} %get-tuple-element.117), channel_id=1, source_target_pairs={{4,0},{8,4},{12,8},{16,12},{20,16},{24,20},{28,24},{5,1},{9,5},{13... | collective-permute-start | bytes 147464 | tf_op jit(solution)/shard_map/ppermute | solution.py:23
  136.6 19.4 %collective-permute-start.9 = (f32[2,64,64]{2,1,0:T(8,128)S(1)}, f32[2,64,64]{2,1,0:T(8,128)S(1)}, u32[]{:S(2)}, u32[]{:S(2)}) collective-permute-start(f32[2,64,64]{2,1,0:T(8,128)S(1)} %fusion.14), channel_id=1, source_target_pairs={{1,0},{2,1},{3,2},{5,4},{6,5},{7,6},{9,8},{10,9},{11,10},{13,12},{... | collective-permute-start | bytes 98312 | tf_op jit(solution)/shard_map/ppermute | solution.py:34
  137.9 18.1 %collective-permute-start.8 = (f32[2,64,64]{2,1,0:T(8,128)S(1)}, f32[2,64,64]{2,1,0:T(8,128)S(1)}, u32[]{:S(2)}, u32[]{:S(2)}) collective-permute-start(f32[2,64,64]{2,1,0:T(8,128)S(1)} %fusion.14), channel_id=1, source_target_pairs={{0,1},{1,2},{2,3},{4,5},{5,6},{6,7},{8,9},{9,10},{10,11},{12,13},{... | collective-permute-start | bytes 98312 | tf_op jit(solution)/shard_map/ppermute | solution.py:33
  151.4 16.5 %copy-start.2 = (f32[2,32,128]{2,1,0:T(8,128)S(1)}, f32[2,32,128]{2,1,0:T(8,128)}, u32[]{:S(2)}) copy-start(f32[2,32,128]{2,1,0:T(8,128)} %param.21) | copy-start | bytes 98308
  152.1 15.8 %all-to-all-start.1 = ((f32[4,3,32,128]{3,2,1,0:T(8,128)}), f32[4,3,32,128]{3,2,1,0:T(8,128)S(1)}, u32[]{:S(2)}, u32[]{:S(2)}) async-start(f32[4,3,32,128]{3,2,1,0:T(8,128)} %copy.33), calls=%async_computation.1 | async-start | bytes 393216 | tf_op jit(solution)/shard_map/all_to_all | solution.py:206
  156.0 10.6 %collective-permute-start.11 = (f32[2,192,64]{2,1,0:T(8,128)S(1)}, f32[2,192,64]{2,1,0:T(8,128)S(1)}, u32[]{:S(2)}, u32[]{:S(2)}) collective-permute-start(f32[2,192,64]{2,1,0:T(8,128)S(1)} %pad_maximum_fusion.4), channel_id=1, source_target_pairs={{4,0},{8,4},{12,8},{16,12},{20,16},{24,20},{28,24},{5,1},{9,5},{13... | collective-permute-start | bytes 294920 | tf_op jit(solution)/shard_map/ppermute | solution.py:34
  157.3 10.3 %collective-permute-start.10 = (f32[2,192,64]{2,1,0:T(8,128)S(1)}, f32[2,192,64]{2,1,0:T(8,128)S(1)}, u32[]{:S(2)}, u32[]{:S(2)}) collective-permute-start(f32[2,192,64]{2,1,0:T(8,128)S(1)} %pad_maximum_fusion.4), channel_id=1, source_target_pairs={{0,4},{4,8},{8,12},{12,16},{16,20},{20,24},{24,28},{1,5},{5,9},{9,... | collective-permute-start | bytes 294920 | tf_op jit(solution)/shard_map/ppermute | solution.py:33
  274.9 24.5 %all-to-all-start.2 = ((f32[8,3,4,32,128]{4,3,2,1,0:T(8,128)}), f32[8,3,4,32,128]{4,3,2,1,0:T(8,128)S(1)}, u32[]{:S(2)}, u32[]{:S(2)}) async-start(f32[8,3,4,32,128]{4,3,2,1,0:T(8,128)} %copy_bitcast_fusion), calls=%async_computation.2 | async-start | bytes 3145728 | tf_op jit(solution)/shard_map/all_to_all | solution.py:204
  278.5 6.3 %collective-permute-start.12 = (f32[3,64,192]{2,1,0:T(8,128)S(1)}, f32[3,64,192]{2,1,0:T(8,128)S(1)}, u32[]{:S(2)}, u32[]{:S(2)}) collective-permute-start(f32[3,64,192]{2,1,0:T(8,128)S(1)} %get-tuple-element.110), channel_id=1, source_target_pairs={{0,1},{1,2},{2,3},{4,5},{5,6},{6,7},{8,9},{9,10},{10,11},{12,13},{... | collective-permute-start | bytes 442376 | tf_op jit(solution)/shard_map/ppermute | solution.py:23
  279.8 9.1 %collective-permute-start.13 = (f32[3,64,192]{2,1,0:T(8,128)S(1)}, f32[3,64,192]{2,1,0:T(8,128)S(1)}, u32[]{:S(2)}, u32[]{:S(2)}) collective-permute-start(f32[3,64,192]{2,1,0:T(8,128)S(1)} %get-tuple-element.111), channel_id=1, source_target_pairs={{1,0},{2,1},{3,2},{5,4},{6,5},{7,6},{9,8},{10,9},{11,10},{13,12},{... | collective-permute-start | bytes 442376 | tf_op jit(solution)/shard_map/ppermute | solution.py:23
  289.0 2.8 collective-permute-start.14
  290.5 4.9 %collective-permute-start.15 = (f32[3,64,64]{2,1,0:T(8,128)S(1)}, f32[3,64,64]{2,1,0:T(8,128)S(1)}, u32[]{:S(2)}, u32[]{:S(2)}) collective-permute-start(f32[3,64,64]{2,1,0:T(8,128)S(1)} %get-tuple-element.115), channel_id=1, source_target_pairs={{4,0},{8,4},{12,8},{16,12},{20,16},{24,20},{28,24},{5,1},{9,5},{13... | collective-permute-start | bytes 147464 | tf_op jit(solution)/shard_map/ppermute | solution.py:23
  300.2 11.2 %all-to-all-start.3 = ((f32[4,3,32,128]{3,2,1,0:T(8,128)}), f32[4,3,32,128]{3,2,1,0:T(8,128)S(1)}, u32[]{:S(2)}, u32[]{:S(2)}) async-start(f32[4,3,32,128]{3,2,1,0:T(8,128)} %copy.37), calls=%async_computation.3 | async-start | bytes 393216 | tf_op jit(solution)/shard_map/all_to_all | solution.py:206

commit v2 on v1

--- a/solution.py
+++ b/solution.py
@@ -189,11 +189,12 @@
 
 
 def whole_of(own):
-    planes = []
-    for plane in own:
-        planes.append(lax.all_gather(plane, ("gy", "gx"), axis=0, tiled=True))
-        own = lax.optimization_barrier(own)
-    return jnp.stack(planes)
+    planes, rows, side = own.shape
+    blocks = own
+    for axis in ("gy", "gx"):
+        copies = jnp.broadcast_to(blocks[None], (lax.axis_size(axis), *blocks.shape))
+        blocks = lax.all_to_all(copies, axis, 0, 0, tiled=True)
+    return blocks.transpose(2, 1, 0, 3, 4).reshape(planes, -1, side)
 
 
 def scattered_sum(terms):

time: 313 us -> 195 us (0.62)
  blocking collectives: 165 us -> 0 us
  waiting for transfers between devices: 35.8 us -> 63.8 us
  starting transfers between devices: 59.1 us -> 72.5 us
  local copies, waits for them, and re-layouts: 3.05 us -> 8.44 us
    all_gather x4 -> x0, blocking collectives: 165 us -> none  [whole_of(): planes.append(lax.all_gather(plane, ('gy', 'gx'), axis=0, tiled=True))]
    all_to_all x0 -> x4, waiting for transfers between devices: none -> 18.9 us  [whole_of(): blocks = lax.all_to_all(copies, axis, 0, 0, tiled=True)]
    all_to_all x0 -> x4, starting transfers between devices: none -> 15.1 us  [whole_of(): blocks = lax.all_to_all(copies, axis, 0, 0, tiled=True)]
    ppermute x4, starting transfers between devices: 22.5 us -> 16.2 us  [extended_2(): before = lax.ppermute(last, axis, up)]
    all_to_all x2, waiting for transfers between devices: 7.14 us -> 13.2 us  [scattered_sum(): return lax.all_to_all(terms, 'gy', 0, 0, tiled=True).sum(axis=0)]
    all_to_all x2, waiting for transfers between devices: 11.3 us -> 16.7 us  [scattered_sum(): terms = lax.all_to_all(terms, 'gx', 0, 0, tiled=True).sum(axis=0)]
    broadcast_in_dim x0 -> x4, local copies, waits for them, and re-layouts: none -> 4.29 us  [whole_of(): jnp.broadcast_to(blocks[None], (lax.axis_size(axis), *blocks.shape))]
    ppermute x8, waiting for transfers between devices: 15.4 us -> 11.4 us  [from_behind(): return lax.ppermute(block, axis, route)]
  transfers between devices with their start and end apart: 20 -> 24, of which waited for: 9 -> 15; matrix products, arithmetic and copies ran while one was open for 2% -> 6% of each run, Pallas kernels for 0% -> 0%
where the time goes in v2:
time: 195 us; the launch traced here: 194 us
  starting transfers between devices  72.5 us (37%)
  waiting for transfers between devices  63.8 us (33%)
  Pallas kernels  40 us (21%)
  local copies, waits for them, and re-layouts  8.44 us (4%)
  other arithmetic  8.1 us (4%)
    pallas_call x2, Pallas kernels, gradients(): pl.pallas_call(visit_kernel, out_shape=(jax.ShapeDtypeStruct((3, rows, la...  40 us
    all_to_all x4, waiting for transfers between devices, whole_of(): blocks = lax.all_to_all(copies, axis, 0, 0, tiled=True)  18.9 us
    all_to_all x2, waiting for transfers between devices, scattered_sum(): terms = lax.all_to_all(terms, 'gx', 0, 0, tiled=True).sum(axis=0)  16.7 us
    ppermute x4, starting transfers between devices, extended_2(): before = lax.ppermute(last, axis, up)  16.2 us
    ppermute x8, starting transfers between devices, from_behind(): return lax.ppermute(block, axis, route)  15.5 us
    all_to_all x4, starting transfers between devices, whole_of(): blocks = lax.all_to_all(copies, axis, 0, 0, tiled=True)  15.1 us
    all_to_all x2, waiting for transfers between devices, scattered_sum(): return lax.all_to_all(terms, 'gy', 0, 0, tiled=True).sum(axis=0)  13.2 us
    all_to_all x2, starting transfers between devices, scattered_sum(): terms = lax.all_to_all(terms, 'gx', 0, 0, tiled=True).sum(axis=0)  12 us
  transfers between devices with their start and end apart: 24, of which 15 were waited for; matrix products, arithmetic and copies ran while one was open for 6% of the time, Pallas kernels for 0%

profile of v2, /device:TPU:0, one launch (start us, length us, event | category | flops | bytes accessed | tf_op | source)
XLA Modules:
  0.0 194.0 jit_solution(10627423148108234133)
XLA Ops:
  1.9 5.6 %collective-permute-start = (f32[2,64,64]{2,1,0:T(8,128)}, f32[2,64,64]{2,1,0:T(8,128)S(1)}, u32[]{:S(2)}, u32[]{:S(2)}) collective-permute-start(f32[2,64,64]{2,1,0:T(8,128)} %param.20), channel_id=1, source_target_pairs={{0,1},{1,2},{2,3},{4,5},{5,6},{6,7},{8,9},{9,10},{10,11},{12,13},{... | collective-permute-start | bytes 98312 | tf_op jit(solution)/shard_map/ppermute | solution.py:33
  7.5 1.4 broadcast_in_dim.8
  8.9 4.3 %all-to-all-start = ((f32[4,2,32,128]{3,2,1,0:T(8,128)}), f32[4,2,32,128]{3,2,1,0:T(8,128)S(1)}, u32[]{:S(2)}, u32[]{:S(2)}) async-start(f32[4,2,32,128]{3,2,1,0:T(8,128)} %broadcast_in_dim.8), calls=%async_computation | async-start | bytes 262144 | tf_op jit(solution)/shard_map/all_to_all | solution.py:196
  14.3 4.9 %all-to-all-done = f32[4,2,32,128]{3,2,1,0:T(8,128)S(1)} async-done(((f32[4,2,32,128]{3,2,1,0:T(8,128)}), f32[4,2,32,128]{3,2,1,0:T(8,128)S(1)}, u32[]{:S(2)}, u32[]{:S(2)}) %all-to-all-start) | async-done | bytes 131104 | tf_op jit(solution)/shard_map/all_to_all | solution.py:196
  20.3 3.9 %all-to-all-start.1 = ((f32[8,4,2,32,128]{4,3,1,2,0:T(8,128)}), f32[8,4,2,32,128]{4,3,1,2,0:T(8,128)S(1)}, u32[]{:S(2)}, u32[]{:S(2)}) async-start(f32[8,4,2,32,128]{4,3,1,2,0:T(8,128)} %broadcast_in_dim.9), calls=%async_computation.1 | async-start | bytes 2097152 | tf_op jit(solution)/shard_map/all_to_all | solution.py:196
  26.3 3.0 %collective-permute-start.2 = (f32[2,192,64]{2,1,0:T(8,128)S(1)}, f32[2,192,64]{2,1,0:T(8,128)S(1)}, u32[]{:S(2)}, u32[]{:S(2)}) collective-permute-start(f32[2,192,64]{2,1,0:T(8,128)S(1)} %constant_dynamic-update-slice_fusion), channel_id=1, source_target_pairs={{0,4},{4,8},{8,12},{12,16},{16,20},{20,24},{24,28},{1,5},{5,9},{9,... | collective-permute-start | bytes 294920 | tf_op jit(solution)/shard_map/ppermute | solution.py:33
  30.6 8.9 %all-to-all-done.1 = f32[8,4,2,32,128]{4,3,1,2,0:T(8,128)S(1)} async-done(((f32[8,4,2,32,128]{4,3,1,2,0:T(8,128)}), f32[8,4,2,32,128]{4,3,1,2,0:T(8,128)S(1)}, u32[]{:S(2)}, u32[]{:S(2)}) %all-to-all-start.1) | async-done | bytes 1048608 | tf_op jit(solution)/shard_map/all_to_all | solution.py:196
  39.6 20.0 %visits.2 = (f32[3,192,256]{2,1,0:T(8,128)S(1)}, f32[2,1024,128]{2,1,0:T(8,128)S(1)}, f32[128,128]{1,0:T(8,128)S(1)}) custom-call(s32[12,2]{1,0:T(8,128)S(1)} %copy.44.places, f32[2,192,256]{2,1,0:T(8,128)S(1)} %select_maximum_fusion.4.ext_ref, f32[2,1024,128]{2,1,0:T(8,128)S(1)} %bitcast.71, f32[12,128,128]{2,1,0:T(8,128)S(1)} %bitcast.80, ...), custom_call_target="tpu_custom_call" | custom-call | flops 6442450944 | bytes 4194304 | tf_op jit(solution)/shard_map/visits/pallas_call | solution.py:152
  59.7 1.4 copy_bitcast_fusion.1
  61.0 5.7 %all-to-all-start.2 = ((f32[8,3,4,32,128]{4,3,2,1,0:T(8,128)}), f32[8,3,4,32,128]{4,3,2,1,0:T(8,128)S(1)}, u32[]{:S(2)}, u32[]{:S(2)}) async-start(f32[8,3,4,32,128]{4,3,2,1,0:T(8,128)} %copy_bitcast_fusion.1), calls=%async_computation.2 | async-start | bytes 3145728 | tf_op jit(solution)/shard_map/all_to_all | solution.py:205
  67.5 3.9 %collective-permute-start.4 = (f32[3,64,192]{2,1,0:T(8,128)}, f32[3,64,192]{2,1,0:T(8,128)}, u32[]{:S(2)}, u32[]{:S(2)}) collective-permute-start(f32[3,64,192]{2,1,0:T(8,128)} %get-tuple-element.112), channel_id=1, source_target_pairs={{0,1},{1,2},{2,3},{4,5},{5,6},{6,7},{8,9},{9,10},{10,11},{12,13},{... | collective-permute-start | bytes 442376 | tf_op jit(solution)/shard_map/ppermute | solution.py:23
  72.6 15.1 %all-to-all-done.2 = f32[8,3,4,32,128]{4,3,2,1,0:T(8,128)S(1)} async-done(((f32[8,3,4,32,128]{4,3,2,1,0:T(8,128)}), f32[8,3,4,32,128]{4,3,2,1,0:T(8,128)S(1)}, u32[]{:S(2)}, u32[]{:S(2)}) %all-to-all-start.2) | async-done | bytes 1572896 | tf_op jit(solution)/shard_map/all_to_all | solution.py:205
  88.5 1.6 copy.47
  90.2 3.4 %all-to-all-start.3 = ((f32[4,3,32,128]{3,2,1,0:T(8,128)}), f32[4,3,32,128]{3,2,1,0:T(8,128)S(1)}, u32[]{:S(2)}, u32[]{:S(2)}) async-start(f32[4,3,32,128]{3,2,1,0:T(8,128)} %copy.47), calls=%async_computation.3 | async-start | bytes 393216 | tf_op jit(solution)/shard_map/all_to_all | solution.py:207
  94.6 5.1 %all-to-all-done.3 = f32[4,3,32,128]{3,2,1,0:T(8,128)S(1)} async-done(((f32[4,3,32,128]{3,2,1,0:T(8,128)}), f32[4,3,32,128]{3,2,1,0:T(8,128)S(1)}, u32[]{:S(2)}, u32[]{:S(2)}) %all-to-all-start.3) | async-done | bytes 196640 | tf_op jit(solution)/shard_map/all_to_all | solution.py:207
  100.5 3.3 %all-to-all-start.4 = ((f32[4,2,32,128]{3,2,1,0:T(8,128)}), f32[4,2,32,128]{3,2,1,0:T(8,128)S(1)}, u32[]{:S(2)}, u32[]{:S(2)}) async-start(f32[4,2,32,128]{3,2,1,0:T(8,128)} %broadcast_in_dim.10), calls=%async_computation.4 | async-start | bytes 262144 | tf_op jit(solution)/shard_map/all_to_all | solution.py:196
  106.4 3.3 %all-to-all-done.4 = f32[4,2,32,128]{3,2,1,0:T(8,128)S(1)} async-done(((f32[4,2,32,128]{3,2,1,0:T(8,128)}), f32[4,2,32,128]{3,2,1,0:T(8,128)S(1)}, u32[]{:S(2)}, u32[]{:S(2)}) %all-to-all-start.4) | async-done | bytes 131104 | tf_op jit(solution)/shard_map/all_to_all | solution.py:196
  110.8 3.6 %all-to-all-start.5 = ((f32[8,4,2,32,128]{4,3,1,2,0:T(8,128)}), f32[8,4,2,32,128]{4,3,1,2,0:T(8,128)S(1)}, u32[]{:S(2)}, u32[]{:S(2)}) async-start(f32[8,4,2,32,128]{4,3,1,2,0:T(8,128)} %broadcast_in_dim.11), calls=%async_computation.5 | async-start | bytes 2097152 | tf_op jit(solution)/shard_map/all_to_all | solution.py:196
  115.8 4.5 %collective-permute-start.8 = (f32[2,64,64]{2,1,0:T(8,128)S(1)}, f32[2,64,64]{2,1,0:T(8,128)S(1)}, u32[]{:S(2)}, u32[]{:S(2)}) collective-permute-start(f32[2,64,64]{2,1,0:T(8,128)S(1)} %fusion.14), channel_id=1, source_target_pairs={{0,1},{1,2},{2,3},{4,5},{5,6},{6,7},{8,9},{9,10},{10,11},{12,13},{... | collective-permute-start | bytes 98312 | tf_op jit(solution)/shard_map/ppermute | solution.py:33
  121.0 1.3 collective-permute-done.8
  123.6 3.0 %collective-permute-start.10 = (f32[2,192,64]{2,1,0:T(8,128)S(1)}, f32[2,192,64]{2,1,0:T(8,128)S(1)}, u32[]{:S(2)}, u32[]{:S(2)}) collective-permute-start(f32[2,192,64]{2,1,0:T(8,128)S(1)} %pad_maximum_fusion.2), channel_id=1, source_target_pairs={{0,4},{4,8},{8,12},{12,16},{16,20},{20,24},{24,28},{1,5},{5,9},{9,... | collective-permute-start | bytes 294920 | tf_op jit(solution)/shard_map/ppermute | solution.py:33
  127.9 1.9 all-to-all-done.5
  129.8 20.0 %visits.3 = (f32[3,192,256]{2,1,0:T(8,128)S(1)}, f32[2,1024,128]{2,1,0:T(8,128)S(1)}, f32[128,128]{1,0:T(8,128)S(1)}) custom-call(s32[12,2]{1,0:T(8,128)S(1)} %copy.44.places, f32[2,192,256]{2,1,0:T(8,128)S(1)} %select_maximum_fusion.ext_ref, f32[2,1024,128]{2,1,0:T(8,128)S(1)} %bitcast.70, f32[12,128,128]{2,1,0:T(8,128)S(1)} %bitcast.81, ...), custom_call_target="tpu_custom_call" | custom-call | flops 6442450944 | bytes 4194304 | tf_op jit(solution)/shard_map/visits/pallas_call | solution.py:152
  149.9 1.4 copy_bitcast_fusion
  151.3 6.3 %all-to-all-start.6 = ((f32[8,3,4,32,128]{4,3,2,1,0:T(8,128)}), f32[8,3,4,32,128]{4,3,2,1,0:T(8,128)S(1)}, u32[]{:S(2)}, u32[]{:S(2)}) async-start(f32[8,3,4,32,128]{4,3,2,1,0:T(8,128)} %copy_bitcast_fusion), calls=%async_computation.6 | async-start | bytes 3145728 | tf_op jit(solution)/shard_map/all_to_all | solution.py:205
  157.6 3.9 %collective-permute-start.12 = (f32[3,64,192]{2,1,0:T(8,128)S(1)}, f32[3,64,192]{2,1,0:T(8,128)S(1)}, u32[]{:S(2)}, u32[]{:S(2)}) collective-permute-start(f32[3,64,192]{2,1,0:T(8,128)S(1)} %get-tuple-element.110), channel_id=1, source_target_pairs={{0,1},{1,2},{2,3},{4,5},{5,6},{6,7},{8,9},{9,10},{10,11},{12,13},{... | collective-permute-start | bytes 442376 | tf_op jit(solution)/shard_map/ppermute | solution.py:23
  162.7 3.5 %collective-permute-done.12 = f32[3,64,192]{2,1,0:T(8,128)S(1)} collective-permute-done((f32[3,64,192]{2,1,0:T(8,128)S(1)}, f32[3,64,192]{2,1,0:T(8,128)S(1)}, u32[]{:S(2)}, u32[]{:S(2)}) %collective-permute-start.12) | collective-permute-done | bytes 147488 | tf_op jit(solution)/shard_map/ppermute | solution.py:23
  166.2 4.1 %collective-permute-done.13 = f32[3,64,192]{2,1,0:T(8,128)S(1)} collective-permute-done((f32[3,64,192]{2,1,0:T(8,128)S(1)}, f32[3,64,192]{2,1,0:T(8,128)S(1)}, u32[]{:S(2)}, u32[]{:S(2)}) %collective-permute-start.13) | collective-permute-done | bytes 147488 | tf_op jit(solution)/shard_map/ppermute | solution.py:23
  173.0 3.7 %collective-permute-done.15 = f32[3,64,64]{2,1,0:T(8,128)S(1)} collective-permute-done((f32[3,64,64]{2,1,0:T(8,128)S(1)}, f32[3,64,64]{2,1,0:T(8,128)S(1)}, u32[]{:S(2)}, u32[]{:S(2)}) %collective-permute-start.15) | collective-permute-done | bytes 49184 | tf_op jit(solution)/shard_map/ppermute | solution.py:23
  176.9 1.6 all-to-all-done.6
  179.4 5.3 %all-to-all-start.7 = ((f32[4,3,32,128]{3,2,1,0:T(8,128)}), f32[4,3,32,128]{3,2,1,0:T(8,128)S(1)}, u32[]{:S(2)}, u32[]{:S(2)}) async-start(f32[4,3,32,128]{3,2,1,0:T(8,128)} %copy.53), calls=%async_computation.7 | async-start | bytes 393216 | tf_op jit(solution)/shard_map/all_to_all | solution.py:207
  185.3 8.1 %all-to-all-done.7 = f32[4,3,32,128]{3,2,1,0:T(8,128)S(1)} async-done(((f32[4,3,32,128]{3,2,1,0:T(8,128)}), f32[4,3,32,128]{3,2,1,0:T(8,128)S(1)}, u32[]{:S(2)}, u32[]{:S(2)}) %all-to-all-start.7) | async-done | bytes 196640 | tf_op jit(solution)/shard_map/all_to_all | solution.py:207
  (83 shorter events, 26.0 us)
Async XLA Ops:
  0.6 24.4 %collective-permute-start.1 = (f32[2,64,64]{2,1,0:T(8,128)}, f32[2,64,64]{2,1,0:T(8,128)S(1)}, u32[]{:S(2)}, u32[]{:S(2)}) collective-permute-start(f32[2,64,64]{2,1,0:T(8,128)} %param.20), channel_id=1, source_target_pairs={{1,0},{2,1},{3,2},{5,4},{6,5},{7,6},{9,8},{10,9},{11,10},{13,12},{... | collective-permute-start | bytes 98312 | tf_op jit(solution)/shard_map/ppermute | solution.py:34
  1.9 23.0 %collective-permute-start = (f32[2,64,64]{2,1,0:T(8,128)}, f32[2,64,64]{2,1,0:T(8,128)S(1)}, u32[]{:S(2)}, u32[]{:S(2)}) collective-permute-start(f32[2,64,64]{2,1,0:T(8,128)} %param.20), channel_id=1, source_target_pairs={{0,1},{1,2},{2,3},{4,5},{5,6},{6,7},{8,9},{9,10},{10,11},{12,13},{... | collective-permute-start | bytes 98312 | tf_op jit(solution)/shard_map/ppermute | solution.py:33
  8.9 10.2 %all-to-all-start = ((f32[4,2,32,128]{3,2,1,0:T(8,128)}), f32[4,2,32,128]{3,2,1,0:T(8,128)S(1)}, u32[]{:S(2)}, u32[]{:S(2)}) async-start(f32[4,2,32,128]{3,2,1,0:T(8,128)} %broadcast_in_dim.8), calls=%async_computation | async-start | bytes 262144 | tf_op jit(solution)/shard_map/all_to_all | solution.py:196
  20.3 4.2 %copy-start.3 = (s32[1,1,12,2]{2,3,1,0:T(2,128)S(1)}, s32[1,1,12,2]{2,3,1,0:T(2,128)}, u32[]{:S(2)}) copy-start(s32[1,1,12,2]{2,3,1,0:T(2,128)} %param.22) | copy-start | bytes 292
  20.3 19.2 %all-to-all-start.1 = ((f32[8,4,2,32,128]{4,3,1,2,0:T(8,128)}), f32[8,4,2,32,128]{4,3,1,2,0:T(8,128)S(1)}, u32[]{:S(2)}, u32[]{:S(2)}) async-start(f32[8,4,2,32,128]{4,3,1,2,0:T(8,128)} %broadcast_in_dim.9), calls=%async_computation.1 | async-start | bytes 2097152 | tf_op jit(solution)/shard_map/all_to_all | solution.py:196
  24.1 0.8 copy-start.1
  25.0 4.7 %collective-permute-start.3 = (f32[2,192,64]{2,1,0:T(8,128)S(1)}, f32[2,192,64]{2,1,0:T(8,128)S(1)}, u32[]{:S(2)}, u32[]{:S(2)}) collective-permute-start(f32[2,192,64]{2,1,0:T(8,128)S(1)} %constant_dynamic-update-slice_fusion), channel_id=1, source_target_pairs={{4,0},{8,4},{12,8},{16,12},{20,16},{24,20},{28,24},{5,1},{9,5},{13... | collective-permute-start | bytes 294920 | tf_op jit(solution)/shard_map/ppermute | solution.py:34
  26.3 4.1 %collective-permute-start.2 = (f32[2,192,64]{2,1,0:T(8,128)S(1)}, f32[2,192,64]{2,1,0:T(8,128)S(1)}, u32[]{:S(2)}, u32[]{:S(2)}) collective-permute-start(f32[2,192,64]{2,1,0:T(8,128)S(1)} %constant_dynamic-update-slice_fusion), channel_id=1, source_target_pairs={{0,4},{4,8},{8,12},{12,16},{16,20},{20,24},{24,28},{1,5},{5,9},{9,... | collective-permute-start | bytes 294920 | tf_op jit(solution)/shard_map/ppermute | solution.py:33
  29.8 9.9 %copy-start = (f32[1,1,12,128,128]{4,3,2,1,0:T(8,128)S(1)}, f32[1,1,12,128,128]{4,3,2,1,0:T(8,128)}, u32[]{:S(2)}) copy-start(f32[1,1,12,128,128]{4,3,2,1,0:T(8,128)} %param.23) | copy-start | bytes 2359300
  61.0 26.7 %all-to-all-start.2 = ((f32[8,3,4,32,128]{4,3,2,1,0:T(8,128)}), f32[8,3,4,32,128]{4,3,2,1,0:T(8,128)S(1)}, u32[]{:S(2)}, u32[]{:S(2)}) async-start(f32[8,3,4,32,128]{4,3,2,1,0:T(8,128)} %copy_bitcast_fusion.1), calls=%async_computation.2 | async-start | bytes 3145728 | tf_op jit(solution)/shard_map/all_to_all | solution.py:205
  67.5 26.0 %collective-permute-start.4 = (f32[3,64,192]{2,1,0:T(8,128)}, f32[3,64,192]{2,1,0:T(8,128)}, u32[]{:S(2)}, u32[]{:S(2)}) collective-permute-start(f32[3,64,192]{2,1,0:T(8,128)} %get-tuple-element.112), channel_id=1, source_target_pairs={{0,1},{1,2},{2,3},{4,5},{5,6},{6,7},{8,9},{9,10},{10,11},{12,13},{... | collective-permute-start | bytes 442376 | tf_op jit(solution)/shard_map/ppermute | solution.py:23
  71.4 22.2 %collective-permute-start.5 = (f32[3,64,192]{2,1,0:T(8,128)}, f32[3,64,192]{2,1,0:T(8,128)}, u32[]{:S(2)}, u32[]{:S(2)}) collective-permute-start(f32[3,64,192]{2,1,0:T(8,128)} %get-tuple-element.113), channel_id=1, source_target_pairs={{1,0},{2,1},{3,2},{5,4},{6,5},{7,6},{9,8},{10,9},{11,10},{13,12},{... | collective-permute-start | bytes 442376 | tf_op jit(solution)/shard_map/ppermute | solution.py:23
  88.5 11.2 %copy-start.2 = (f32[2,32,128]{2,1,0:T(8,128)S(1)}, f32[2,32,128]{2,1,0:T(8,128)}, u32[]{:S(2)}) copy-start(f32[2,32,128]{2,1,0:T(8,128)} %param.21) | copy-start | bytes 98308
  90.2 9.6 %all-to-all-start.3 = ((f32[4,3,32,128]{3,2,1,0:T(8,128)}), f32[4,3,32,128]{3,2,1,0:T(8,128)S(1)}, u32[]{:S(2)}, u32[]{:S(2)}) async-start(f32[4,3,32,128]{3,2,1,0:T(8,128)} %copy.47), calls=%async_computation.3 | async-start | bytes 393216 | tf_op jit(solution)/shard_map/all_to_all | solution.py:207
  100.5 9.2 %all-to-all-start.4 = ((f32[4,2,32,128]{3,2,1,0:T(8,128)}), f32[4,2,32,128]{3,2,1,0:T(8,128)S(1)}, u32[]{:S(2)}, u32[]{:S(2)}) async-start(f32[4,2,32,128]{3,2,1,0:T(8,128)} %broadcast_in_dim.10), calls=%async_computation.4 | async-start | bytes 262144 | tf_op jit(solution)/shard_map/all_to_all | solution.py:196
  103.8 10.6 %collective-permute-start.6 = (f32[3,64,64]{2,1,0:T(8,128)S(1)}, f32[3,64,64]{2,1,0:T(8,128)S(1)}, u32[]{:S(2)}, u32[]{:S(2)}) collective-permute-start(f32[3,64,64]{2,1,0:T(8,128)S(1)} %get-tuple-element.116), channel_id=1, source_target_pairs={{0,4},{4,8},{8,12},{12,16},{16,20},{20,24},{24,28},{1,5},{5,9},{9,... | collective-permute-start | bytes 147464 | tf_op jit(solution)/shard_map/ppermute | solution.py:23
  105.1 9.3 %collective-permute-start.7 = (f32[3,64,64]{2,1,0:T(8,128)S(1)}, f32[3,64,64]{2,1,0:T(8,128)S(1)}, u32[]{:S(2)}, u32[]{:S(2)}) collective-permute-start(f32[3,64,64]{2,1,0:T(8,128)S(1)} %get-tuple-element.117), channel_id=1, source_target_pairs={{4,0},{8,4},{12,8},{16,12},{20,16},{24,20},{28,24},{5,1},{9,5},{13... | collective-permute-start | bytes 147464 | tf_op jit(solution)/shard_map/ppermute | solution.py:23
  110.8 19.0 %all-to-all-start.5 = ((f32[8,4,2,32,128]{4,3,1,2,0:T(8,128)}), f32[8,4,2,32,128]{4,3,1,2,0:T(8,128)S(1)}, u32[]{:S(2)}, u32[]{:S(2)}) async-start(f32[8,4,2,32,128]{4,3,1,2,0:T(8,128)} %broadcast_in_dim.11), calls=%async_computation.5 | async-start | bytes 2097152 | tf_op jit(solution)/shard_map/all_to_all | solution.py:196
  114.5 6.4 %collective-permute-start.9 = (f32[2,64,64]{2,1,0:T(8,128)S(1)}, f32[2,64,64]{2,1,0:T(8,128)S(1)}, u32[]{:S(2)}, u32[]{:S(2)}) collective-permute-start(f32[2,64,64]{2,1,0:T(8,128)S(1)} %fusion.14), channel_id=1, source_target_pairs={{1,0},{2,1},{3,2},{5,4},{6,5},{7,6},{9,8},{10,9},{11,10},{13,12},{... | collective-permute-start | bytes 98312 | tf_op jit(solution)/shard_map/ppermute | solution.py:34
  115.8 6.4 %collective-permute-start.8 = (f32[2,64,64]{2,1,0:T(8,128)S(1)}, f32[2,64,64]{2,1,0:T(8,128)S(1)}, u32[]{:S(2)}, u32[]{:S(2)}) collective-permute-start(f32[2,64,64]{2,1,0:T(8,128)S(1)} %fusion.14), channel_id=1, source_target_pairs={{0,1},{1,2},{2,3},{4,5},{5,6},{6,7},{8,9},{9,10},{10,11},{12,13},{... | collective-permute-start | bytes 98312 | tf_op jit(solution)/shard_map/ppermute | solution.py:33
  122.3 4.4 %collective-permute-start.11 = (f32[2,192,64]{2,1,0:T(8,128)S(1)}, f32[2,192,64]{2,1,0:T(8,128)S(1)}, u32[]{:S(2)}, u32[]{:S(2)}) collective-permute-start(f32[2,192,64]{2,1,0:T(8,128)S(1)} %pad_maximum_fusion.2), channel_id=1, source_target_pairs={{4,0},{8,4},{12,8},{16,12},{20,16},{24,20},{28,24},{5,1},{9,5},{13... | collective-permute-start | bytes 294920 | tf_op jit(solution)/shard_map/ppermute | solution.py:34
  123.6 4.1 %collective-permute-start.10 = (f32[2,192,64]{2,1,0:T(8,128)S(1)}, f32[2,192,64]{2,1,0:T(8,128)S(1)}, u32[]{:S(2)}, u32[]{:S(2)}) collective-permute-start(f32[2,192,64]{2,1,0:T(8,128)S(1)} %pad_maximum_fusion.2), channel_id=1, source_target_pairs={{0,4},{4,8},{8,12},{12,16},{16,20},{20,24},{24,28},{1,5},{5,9},{9,... | collective-permute-start | bytes 294920 | tf_op jit(solution)/shard_map/ppermute | solution.py:33
  151.3 27.3 %all-to-all-start.6 = ((f32[8,3,4,32,128]{4,3,2,1,0:T(8,128)}), f32[8,3,4,32,128]{4,3,2,1,0:T(8,128)S(1)}, u32[]{:S(2)}, u32[]{:S(2)}) async-start(f32[8,3,4,32,128]{4,3,2,1,0:T(8,128)} %copy_bitcast_fusion), calls=%async_computation.6 | async-start | bytes 3145728 | tf_op jit(solution)/shard_map/all_to_all | solution.py:205
  157.6 8.7 %collective-permute-start.12 = (f32[3,64,192]{2,1,0:T(8,128)S(1)}, f32[3,64,192]{2,1,0:T(8,128)S(1)}, u32[]{:S(2)}, u32[]{:S(2)}) collective-permute-start(f32[3,64,192]{2,1,0:T(8,128)S(1)} %get-tuple-element.110), channel_id=1, source_target_pairs={{0,1},{1,2},{2,3},{4,5},{5,6},{6,7},{8,9},{9,10},{10,11},{12,13},{... | collective-permute-start | bytes 442376 | tf_op jit(solution)/shard_map/ppermute | solution.py:23
  161.4 8.9 %collective-permute-start.13 = (f32[3,64,192]{2,1,0:T(8,128)S(1)}, f32[3,64,192]{2,1,0:T(8,128)S(1)}, u32[]{:S(2)}, u32[]{:S(2)}) collective-permute-start(f32[3,64,192]{2,1,0:T(8,128)S(1)} %get-tuple-element.111), channel_id=1, source_target_pairs={{1,0},{2,1},{3,2},{5,4},{6,5},{7,6},{9,8},{10,9},{11,10},{13,12},{... | collective-permute-start | bytes 442376 | tf_op jit(solution)/shard_map/ppermute | solution.py:23
  170.4 2.6 %collective-permute-start.14 = (f32[3,64,64]{2,1,0:T(8,128)S(1)}, f32[3,64,64]{2,1,0:T(8,128)S(1)}, u32[]{:S(2)}, u32[]{:S(2)}) collective-permute-start(f32[3,64,64]{2,1,0:T(8,128)S(1)} %get-tuple-element.114), channel_id=1, source_target_pairs={{0,4},{4,8},{8,12},{12,16},{16,20},{20,24},{24,28},{1,5},{5,9},{9,... | collective-permute-start | bytes 147464 | tf_op jit(solution)/shard_map/ppermute | solution.py:23
  171.7 5.1 %collective-permute-start.15 = (f32[3,64,64]{2,1,0:T(8,128)S(1)}, f32[3,64,64]{2,1,0:T(8,128)S(1)}, u32[]{:S(2)}, u32[]{:S(2)}) collective-permute-start(f32[3,64,64]{2,1,0:T(8,128)S(1)} %get-tuple-element.115), channel_id=1, source_target_pairs={{4,0},{8,4},{12,8},{16,12},{20,16},{24,20},{28,24},{5,1},{9,5},{13... | collective-permute-start | bytes 147464 | tf_op jit(solution)/shard_map/ppermute | solution.py:23
  179.4 14.0 %all-to-all-start.7 = ((f32[4,3,32,128]{3,2,1,0:T(8,128)}), f32[4,3,32,128]{3,2,1,0:T(8,128)S(1)}, u32[]{:S(2)}, u32[]{:S(2)}) async-start(f32[4,3,32,128]{3,2,1,0:T(8,128)} %copy.53), calls=%async_computation.7 | async-start | bytes 393216 | tf_op jit(solution)/shard_map/all_to_all | solution.py:207
